TPU v7x, 128 devices: a whole 4x4x4 slice. The times are simulated.
128 devices in a mesh: member: 8 (over y, core), shard: 16 (over z, x).
Axes of the slice: x: 4, y: 4, z: 4, core: 2. Of those that a mesh axis runs over, the one named last changes fastest.
Arguments:
- member_grams: float32 [8, 4096, 4096], P('member', 'shard'), as said below
- member_weights: bfloat16 [8, 4096, 2304], P('member', 'shard'), may hold values from -6 to 6
Outputs:
- merged: float32 [4096, 2304], P('shard', 'member')
Inputs may be any that keep to these rules, and one draw needn't show every extreme that they name: `member_grams`: each member's matrix is symmetric positive definite.
All inputs are finite; a program needn't handle non-finite values.
Results may differ from a plain program's by a relative error of at most 0.0032.
Values may be sent and summed in bfloat16 or wider, within the bound.
No kernel may reach another device: no remote copies, remote signals or barrier semaphores. Data moves between devices by JAX's collectives and lax.ppermute only.
A program may use at most 128 MiB of HBM per device.

v0:
```python
import jax
import jax.numpy as jnp
from jax import lax
from jax.sharding import PartitionSpec as P

ITERS = 3


shrink = 0.9


def copy_for_each(shard, axis):
    copies = jnp.broadcast_to(shard, (lax.axis_size(axis), *shard.shape))
    return lax.all_to_all(copies, axis, split_axis=0, concat_axis=0, tiled=True)


def taken_together(shard, axis):
    everything = copy_for_each(shard, axis)
    return jnp.sum(everything, axis=0)


def packed_total(arrays, axis):
    ends = [0]
    for a in arrays:
        ends.append(ends[-1] + a.size)
    subtotal = taken_together(jnp.concatenate([a.ravel() for a in arrays]), axis)
    return tuple((subtotal[b:e].reshape(a.shape) for a, b, e in zip(arrays, ends, ends[1:])))


def split_up(shard, dim, devices):
    before, after = (shard.shape[:dim], shard.shape[dim + 1 :])
    return jnp.moveaxis(shard.reshape(*before, devices, -1, *after), dim, 0)


def sent_and_summed(shard, axis, dim):
    parts = split_up(shard, dim, lax.axis_size(axis))
    arrived = lax.all_to_all(parts, axis, split_axis=0, concat_axis=0, tiled=True)
    return arrived.sum(axis=0)


def regularize(gram_block, row_offset):
    height = gram_block.shape[-2]
    width = gram_block.shape[-1]
    row_index = lax.broadcasted_iota(jnp.int32, (height, width), 0) + row_offset
    col_index = lax.broadcasted_iota(jnp.int32, (height, width), 1)
    return jnp.where(row_index == col_index, gram_block, shrink * gram_block)


def paired_sums(residual, images):
    return packed_total(
        (jnp.sum(residual * residual, axis=0), jnp.sum(residual * images, axis=0)), "shard"
    )


def shards(member_grams, member_weights):
    height = member_grams.shape[1]
    regular = regularize(member_grams, lax.axis_index("shard") * height)
    gram_low = regular.astype(jnp.bfloat16)
    gram_sum = lax.psum(jnp.sum(regular, axis=0), "member")
    partial_rhs = jnp.einsum(
        "mrn,mno->ro",
        gram_low,
        lax.all_gather(member_weights, "shard", axis=1, tiled=True),
        preferred_element_type=jnp.float32,
    )
    right_side = sent_and_summed(partial_rhs, "member", 1)

    def apply_gram(direction):
        return jnp.dot(
            gram_sum,
            lax.all_gather(direction, "shard", axis=0, tiled=True),
            precision=lax.Precision.HIGHEST,
            preferred_element_type=jnp.float32,
        )

    merged = jnp.zeros_like(right_side)
    residual = right_side
    images = apply_gram(residual)
    norm_now, curvature = paired_sums(residual, images)
    step_size = norm_now / curvature
    direction = residual
    image_dir = images
    for iteration in range(ITERS):
        merged = merged + step_size * direction
        residual = residual - step_size * image_dir
        if iteration + 1 < ITERS:
            images = apply_gram(residual)
            norm_next, curvature = paired_sums(residual, images)
            momentum = norm_next / norm_now
            step_size = norm_next / (curvature - momentum * norm_next / step_size)
            direction = residual + momentum * direction
            image_dir = images + momentum * image_dir
            norm_now = norm_next
    return merged


def solution(mesh):
    return jax.shard_map(
        shards,
        mesh=mesh,
        in_specs=(P("member", "shard", None), P("member", "shard", None)),
        out_specs=P("shard", "member"),
        check_vma=False,
    )
```

profile of v0, /device:TPU:24, one launch (start us, length us, event | category | flops | bytes accessed | tf_op | source)
XLA Modules:
  0.0 445.5 jit_solution(8371773702980375699)
XLA Ops:
  7.4 0.7 all-gather.5.cloned.1.call-update
  8.1 0.0 all-reduce.2.cloned.1.call-start
  8.2 4.9 %fusion = f32[256,4096]{1,0:T(8,128)} fusion(f32[1,256,4096]{2,1,0:T(8,128)} %param.2, s32[256]{0:T(256)S(1)} %iota_add_fusion), kind=kLoop, calls=%fused_computation.2 | loop fusion | flops 3145728 | bytes 8389632 | tf_op jit(solution)/shard_map/reduce_sum | solution.py:59
  13.1 0.0 all-reduce.2.cloned.1.call-update
  13.1 0.0 all-gather.7.cloned.1.call-start
  13.1 121.4 %all-gather.5.cloned.1.call-done = bf16[1,4096,2304]{2,1,0:T(8,128)(2,1)} async-done(((bf16[1,256,2304]{2,1,0:T(8,128)(2,1)}), bf16[1,4096,2304]{2,1,0:T(8,128)(2,1)}) %all-gather.5.cloned.1.call-update) | async-done | bytes 18874384 | tf_op jit(solution)/shard_map/all_gather | solution.py:63
  134.5 23.2 %copy.5 = bf16[2304,4096]{1,0:T(8,128)(2,1)} copy(bf16[2304,4096]{0,1:T(8,128)(2,1)} %bitcast.21) | data formatting | bytes 37748736 | tf_op jit(solution)/shard_map/mrn,mno->ro/dot_general | solution.py:60
  157.7 10.6 %fusion.7 = f32[8,256,288]{1,2,0:T(8,128)S(1)} fusion(bf16[8,288,4096]{2,1,0:T(8,128)(2,1)} %bitcast.22, f32[1,256,4096]{2,1,0:T(8,128)} %param.2, s32[256]{0:T(256)S(1)} %iota_add_fusion), kind=kOutput, calls=%fused_computation.8 | convolution fusion | flops 4836032512 | bytes 25428992 | tf_op jit(solution)/shard_map/mrn,mno->ro/dot_general | solution.py:60
  168.3 32.5 %all_to_all.23 = f32[8,256,288]{1,2,0:T(8,128)S(1)} all-to-all(f32[8,256,288]{1,2,0:T(8,128)S(1)} %fusion.7), channel_id=1, replica_groups=mesh['member'=8,'shard'=16] {'member'}, dimensions={0} | all-to-all | bytes 4718592 | tf_op jit(solution)/shard_map/all_to_all | solution.py:37
  200.8 0.9 reduce_sum.96
  201.7 0.0 all-gather.7.cloned.1.call-update
  201.7 0.0 all-gather.9.cloned.1.call-start
  201.8 0.0 all-reduce.2.cloned.1.call-done
  201.8 58.8 %all-gather.7.cloned.1.call-done = f32[4096,288]{0,1:T(8,128)} async-done(((f32[256,288]{0,1:T(8,128)}), f32[4096,288]{0,1:T(8,128)}) %all-gather.7.cloned.1.call-update) | async-done | bytes 4718608 | tf_op jit(solution)/shard_map/all_gather | solution.py:71
  260.6 7.6 %multiply_reduce_fusion.4 = (f32[288]{0:T(512)S(1)}, f32[288]{0:T(512)S(1)}, f32[256,288]{0,1:T(8,128)S(1)}) fusion(f32[256,288]{0,1:T(8,128)} %reduce_sum.96, f32[256,4096]{1,0:T(8,128)} %all-reduce.2.cloned.1.call-done, f32[4096,288]{0,1:T(8,128)} %all-gather.7.cloned.1.call-done), kind=kOutput, calls=%fused_computation.18 | convolution fusion | flops 3624173056 | bytes 9505024 | tf_op jit(solution)/shard_map/dot_general | solution.py:69
  268.2 0.1 pad_maximum_fusion
  268.3 12.4 %all_to_all.24 = f32[16,1,576]{2,1,0:T(1,128)S(1)} all-to-all(f32[16,1,576]{2,1,0:T(1,128)S(1)} %broadcast_in_dim.8), channel_id=1, replica_groups=mesh['member'=8,'shard'=16] {'shard'}, dimensions={0} | all-to-all | bytes 73728 | tf_op jit(solution)/shard_map/all_to_all | solution.py:14
  280.7 0.1 slice_divide_fusion.1
  280.8 0.8 multiply_subtract_fusion.1
  281.7 0.2 all-gather.11.cloned.1.call-start
  281.9 57.0 %all-gather.9.cloned.1.call-done = f32[4096,288]{0,1:T(8,128)} async-done(((f32[256,288]{0,1:T(8,128)}), f32[4096,288]{0,1:T(8,128)}) %all-gather.9.cloned.1.call-update) | async-done | bytes 4718608 | tf_op jit(solution)/shard_map/all_gather | solution.py:71
  338.9 7.6 %multiply_reduce_fusion.2 = (f32[288]{0:T(512)S(1)}, f32[288]{0:T(512)S(1)}, f32[256,288]{0,1:T(8,128)S(1)}) fusion(f32[256,288]{0,1:T(8,128)} %multiply_subtract_fusion.1, f32[256,4096]{1,0:T(8,128)} %all-reduce.2.cloned.1.call-done, f32[4096,288]{0,1:T(8,128)} %all-gather.9.cloned.1.call-done), kind=kOutput, calls=%fused_computation.15 | convolution fusion | flops 3624173056 | bytes 9505024 | tf_op jit(solution)/shard_map/dot_general | solution.py:69
  346.5 0.1 pad_maximum_fusion.1
  346.6 12.4 %all_to_all.25 = f32[16,1,576]{2,1,0:T(1,128)S(1)} all-to-all(f32[16,1,576]{2,1,0:T(1,128)S(1)} %broadcast_in_dim.9), channel_id=1, replica_groups=mesh['member'=8,'shard'=16] {'shard'}, dimensions={0} | all-to-all | bytes 73728 | tf_op jit(solution)/shard_map/all_to_all | solution.py:14
  359.0 0.1 slice_divide_fusion.3
  359.1 0.9 multiply_reduce_fusion
  360.0 57.2 %all-gather.11.cloned.1.call-done = f32[4096,288]{0,1:T(8,128)} async-done(((f32[256,288]{0,1:T(8,128)}), f32[4096,288]{0,1:T(8,128)}) %all-gather.11.cloned.1.call-update) | async-done | bytes 4718608 | tf_op jit(solution)/shard_map/all_gather | solution.py:71
  417.2 7.6 %fusion.10 = f32[288]{0:T(512)S(1)} fusion(f32[256,288]{0,1:T(8,128)} %get-tuple-element.12, f32[256,4096]{1,0:T(8,128)} %all-reduce.2.cloned.1.call-done, f32[4096,288]{0,1:T(8,128)} %all-gather.11.cloned.1.call-done), kind=kOutput, calls=%fused_computation.10 | convolution fusion | flops 3624025856 | bytes 9208960 | tf_op jit(solution)/shard_map/dot_general | solution.py:69
  424.8 0.1 pad_maximum_fusion.2
  424.9 12.4 %all_to_all.26 = f32[16,1,576]{2,1,0:T(1,128)S(1)} all-to-all(f32[16,1,576]{2,1,0:T(1,128)S(1)} %broadcast_in_dim.10), channel_id=1, replica_groups=mesh['member'=8,'shard'=16] {'shard'}, dimensions={0} | all-to-all | bytes 73728 | tf_op jit(solution)/shard_map/all_to_all | solution.py:14
  437.3 0.1 subtract_divide_fusion
  437.4 1.0 multiply_add_fusion
  (16 shorter events, 0.3 us)
Async XLA Ops:
  7.4 127.1 %all-gather.5.cloned.1.call-start = ((), (), s32[]{:S(2)}) async-start(), calls=%async_computation.4 | async-start | bytes 20054016 | tf_op jit(solution)/shard_map/all_gather | solution.py:63
  8.1 193.7 %all-reduce.2.cloned.1.call-start = ((), (), s32[]{:S(2)}) async-start(), calls=%async_computation.5 | async-start | bytes 8388608 | tf_op jit(solution)/shard_map/psum | solution.py:59
  13.1 247.5 %all-gather.7.cloned.1.call-start = ((), (), s32[]{:S(2)}) async-start(), calls=%async_computation.6 | async-start | bytes 5013504 | tf_op jit(solution)/shard_map/all_gather | solution.py:71
  201.7 79.1 %copy-start = (f32[256,288]{0,1:T(8,128)S(1)}, f32[256,288]{0,1:T(8,128)}, u32[]{:S(2)}) copy-start(f32[256,288]{0,1:T(8,128)} %reduce_sum.96) | copy-start | bytes 884740
  201.7 137.1 %all-gather.9.cloned.1.call-start = ((), (), s32[]{:S(2)}) async-start(), calls=%async_computation.7 | async-start | bytes 5013504 | tf_op jit(solution)/shard_map/all_gather | solution.py:71
  281.7 77.4 %copy-start.1 = (f32[256,288]{0,1:T(8,128)S(1)}, f32[256,288]{0,1:T(8,128)}, u32[]{:S(2)}) copy-start(f32[256,288]{0,1:T(8,128)} %multiply_subtract_fusion.1) | copy-start | bytes 884740
  281.7 135.5 %all-gather.11.cloned.1.call-start = ((), (), s32[]{:S(2)}) async-start(), calls=%async_computation.8 | async-start | bytes 5013504 | tf_op jit(solution)/shard_map/all_gather | solution.py:71
  360.0 77.4 %copy-start.2 = (f32[256,288]{0,1:T(8,128)S(1)}, f32[256,288]{0,1:T(8,128)}, u32[]{:S(2)}) copy-start(f32[256,288]{0,1:T(8,128)} %get-tuple-element.12) | copy-start | bytes 884740
Sparse Core Ops, SparseCore 0:
  10.3 124.1 all-gather.4
  201.8 58.7 all-gather.6
  281.8 57.0 all-gather.8
  360.1 57.0 all-gather.10
Sparse Core Ops, SparseCore 1:
  13.2 73.2 all-reduce.1
where the time goes:
time: 447 us; the launch traced here: 445 us
  waiting for transfers between devices  295 us (66%)
  blocking collectives  69.6 us (16%)
  matrix products  33.4 us (7%)
  local copies, waits for them, and re-layouts  23.3 us (5%)
  between operations  14.7 us (3%)
  other arithmetic  9.03 us (2%)
    all_gather x3, waiting for transfers between devices, apply_gram(): lax.all_gather(direction, 'shard', axis=0, tiled=True)  173 us
    all_gather x1, waiting for transfers between devices, shards(): lax.all_gather(member_weights, 'shard', axis=1, tiled=True)  121 us
    all_to_all x3, blocking collectives, copy_for_each(): return lax.all_to_all(copies, axis, split_axis=0, concat_axis=0, tiled=True)  37.1 us
    all_to_all x1, blocking collectives, sent_and_summed(): lax.all_to_all(parts, axis, split_axis=0, concat_axis=0, tiled=True)  32.5 us
    dot_general x1, local copies, waits for them, and re-layouts, shards(): jnp.einsum('mrn,mno->ro', gram_low, lax.all_gather(member_weights, 'shard...  23.2 us
    dot_general x3, matrix products, apply_gram(): jnp.dot(gram_sum, lax.all_gather(direction, 'shard', axis=0, tiled=True),...  22.9 us
    dot_general x1, matrix products, shards(): jnp.einsum('mrn,mno->ro', gram_low, lax.all_gather(member_weights, 'shard...  10.6 us
  transfers between devices with their start and end apart: 5, of which 4 were waited for; matrix products, arithmetic and copies ran while one was open for 9% of the time, Pallas kernels for 0%

commit v1 on v0

v1 whole, which is shorter than its diff:
```python
import functools
import jax
import jax.numpy as jnp
from jax import lax
from jax.experimental import pallas as pl
from jax.experimental.pallas import tpu as pltpu
from jax.sharding import Mesh, PartitionSpec as P

MEMBER = ("y", "core")
SHARD = ("z", "x")
ALL = ("y", "core", "z", "x")
SIZES = (4, 2, 4, 4)
SHRINK = 0.9
ROWS = 256
CHUNK = 512
COLS = 144
SPARE = 8
F32 = jnp.float32
BF16 = jnp.bfloat16


def exchange(parts, axis):
    return lax.all_to_all(parts, axis, split_axis=0, concat_axis=0, tiled=True)


def turn(block, axis, step):
    size = lax.axis_size(axis)
    return lax.ppermute(block, axis, [(i, (i + step) % size) for i in range(size)])


def dot(a, b):
    return jnp.dot(a, b, preferred_element_type=F32)


def spread_grams(gram, place):
    row = lax.broadcasted_iota(jnp.int32, gram.shape, 0) + place * ROWS
    col = lax.broadcasted_iota(jnp.int32, gram.shape, 1)
    on = row == col
    regular = jnp.where(on, gram, SHRINK * gram)
    low = regular.astype(BF16)
    rest = jnp.sum(jnp.where(on, regular - low.astype(F32), 0.0), axis=0, keepdims=True)
    rest = jnp.pad(rest, ((0, SPARE - 1), (0, 0))).astype(BF16)
    blocks = jnp.concatenate([low, rest], axis=0)
    return blocks.reshape(ROWS + SPARE, -1, CHUNK).transpose(1, 0, 2)


def sum_grams(blocks, place, chunk):
    total = jnp.sum(blocks.astype(F32), axis=0)
    block, rest = total[:ROWS], total[ROWS : ROWS + 1]
    row = lax.broadcasted_iota(jnp.int32, block.shape, 0) + place * ROWS
    col = lax.broadcasted_iota(jnp.int32, block.shape, 1) + chunk * CHUNK
    low = block.astype(BF16)
    rest = rest + jnp.sum(jnp.where(row == col, block - low.astype(F32), 0.0), axis=0, keepdims=True)
    rest = jnp.pad(rest, ((0, SPARE - 1), (0, 0))).astype(BF16)
    return jnp.concatenate([low, rest], axis=0)


def right_side_kernel(w_ref, g_ref, out_ref):
    total = dot(w_ref[0], g_ref[0, :ROWS])
    for m in range(1, w_ref.shape[0]):
        total += dot(w_ref[m], g_ref[m, :ROWS])
    out_ref[...] = total.astype(BF16).reshape(out_ref.shape)


def right_side_parts(weights, grams):
    members, outs, _ = weights.shape
    step = 4
    return pl.pallas_call(
        right_side_kernel,
        grid=(outs // (step * COLS),),
        in_specs=[
            pl.BlockSpec((members, step * COLS, ROWS), lambda i: (0, i, 0)),
            pl.BlockSpec(grams.shape, lambda i: (0, 0, 0)),
        ],
        out_specs=pl.BlockSpec((step, COLS, CHUNK), lambda i: (i, 0, 0)),
        out_shape=jax.ShapeDtypeStruct((outs // COLS, COLS, CHUNK), BF16),
        name="right_side",
    )(weights, grams)


def product_kernel(pos_ref, gram_ref, diag_ref, own_ref, *refs):
    blocks, out_ref = refs[:-1], refs[-1]
    y, core = pos_ref[0], pos_ref[1]
    own = own_ref[...]
    total = jnp.zeros(own.shape, F32)
    for i, ref in enumerate(blocks):
        at = lax.rem(y + 4 - i % 4, 4) * 2 + (core if i < 4 else 1 - core)
        for half in range(2):
            total += dot(ref[:, half * ROWS : (half + 1) * ROWS], gram_ref[2 * at + half, :ROWS])
    out_ref[...] = total + diag_ref[0:1] * (own - blocks[0][...].astype(F32)) + diag_ref[1:2] * own


def apply_gram(pos, grams, diag, own, blocks):
    return pl.pallas_call(
        product_kernel,
        in_specs=[pl.BlockSpec(memory_space=pltpu.SMEM)] + [pl.BlockSpec(memory_space=pltpu.VMEM)] * (3 + len(blocks)),
        out_specs=pl.BlockSpec(memory_space=pltpu.VMEM),
        out_shape=jax.ShapeDtypeStruct(own.shape, F32),
        name="apply_gram",
    )(pos, grams, diag, own, *blocks)


def gather(block):
    mine = [block] + [turn(block, "y", step) for step in (1, 2, 3)]
    return mine + [turn(b, "core", 1) for b in mine]


def to_output(block):
    index = lambda y, core, z, x: ((y * 2 + core) * 4 + z) * 4 + x
    places = [(y, c, z, x) for y in range(4) for c in range(2) for z in range(4) for x in range(4)]
    odd = lax.axis_index("x") % 2
    halves = [block[:, :ROWS], block[:, ROWS:]]
    came = []
    for a in range(2):
        pairs = [
            (index(y, c, z, x), index(z, x // 2, y, 2 * c + ((x % 2) ^ a))) for y, c, z, x in places
        ]
        sent = jnp.where(odd == a, halves[0], halves[1])
        came.append(lax.ppermute(sent, ALL, pairs))
    first = jnp.where(odd == 0, came[0], came[1])
    second = jnp.where(odd == 0, came[1], came[0])
    return jnp.concatenate([first, second], axis=0).T


def column_sums(a, b):
    return jnp.sum(a * b, axis=1, keepdims=True)


def whole_sums(left, right):
    return sum(column_sums(a, b) for a, b in zip(left, right))


def shards(member_grams, member_weights):
    y, core = lax.axis_index("y"), lax.axis_index("core")
    chunk = lax.axis_index(MEMBER)
    place = lax.axis_index(SHARD)
    pos = jnp.stack([y, core]).astype(jnp.int32)

    weights = lax.all_gather(member_weights[0].T, MEMBER, axis=0)
    grams = exchange(spread_grams(member_grams[0], place), MEMBER)
    gram_sum = lax.all_gather(sum_grams(grams, place, chunk), SHARD, axis=0)
    parts = exchange(right_side_parts(weights, grams), SHARD)
    r0 = jnp.sum(parts.astype(F32), axis=0)

    near = lax.dynamic_slice(gram_sum, (2 * chunk, 0, 0), (2, ROWS + SPARE, CHUNK)).astype(F32)
    row = lax.broadcasted_iota(jnp.int32, (ROWS, ROWS), 0)
    col = lax.broadcasted_iota(jnp.int32, (ROWS, ROWS), 1)
    diag = jnp.concatenate(
        [
            jnp.sum(jnp.where(row == col, near[h, :ROWS, h * ROWS : (h + 1) * ROWS], 0.0), axis=0)
            for h in range(2)
        ]
    )
    diag = jnp.stack([diag, near[0, ROWS] + near[1, ROWS]])
    diag = jnp.pad(diag, ((0, 6), (0, 0)))

    def product(own):
        blocks = gather(own.astype(BF16))
        return apply_gram(pos, gram_sum, diag, own, blocks), [b.astype(F32) for b in blocks]

    w0, r0_all = product(r0)
    z0, w0_all = product(w0)
    norm0 = whole_sums(r0_all, r0_all)
    step0 = norm0 / whole_sums(r0_all, w0_all)
    r1 = r0 - step0 * w0
    w1 = w0 - step0 * z0
    q1, w1_all = product(w1)
    r1_all = [r - step0 * w for r, w in zip(r0_all, w0_all)]
    norm1 = whole_sums(r1_all, r1_all)
    beta1 = norm1 / norm0
    step1 = norm1 / (whole_sums(r1_all, w1_all) - beta1 * norm1 / step0)
    s1 = w1 + beta1 * w0
    z1 = q1 + beta1 * z0
    p1 = r1 + beta1 * r0
    r2 = r1 - step1 * s1
    w2 = w1 - step1 * z1
    both = jnp.concatenate([column_sums(r2, r2), column_sums(r2, w2)], axis=1).T
    both = jnp.sum(exchange(jnp.broadcast_to(both, (8, 1, 2, COLS)), MEMBER), axis=(0, 1))
    norm2, curve2 = both[0][:, None], both[1][:, None]
    beta2 = norm2 / norm1
    step2 = norm2 / (curve2 - beta2 * norm2 / step1)
    p2 = r2 + beta2 * p1
    return to_output(step0 * r0 + step1 * p1 + step2 * p2)


def solution(mesh):
    fine = Mesh(mesh.devices.reshape(SIZES), ALL)
    return jax.shard_map(
        shards,
        mesh=fine,
        in_specs=(P(MEMBER, SHARD, None), P(MEMBER, SHARD, None)),
        out_specs=P(SHARD, MEMBER),
        check_vma=False,
    )
```

time: 447 us -> 267 us (0.60)
  waiting for transfers between devices: 295 us -> 147 us
  blocking collectives: 69.6 us -> 0 us
  starting transfers between devices: 0.35 us -> 38.8 us
  matrix products: 33.4 us -> 0 us
  Pallas kernels: 0 us -> 22.2 us
  other arithmetic: 9.03 us -> 27.1 us
  local copies, waits for them, and re-layouts: 23.3 us -> 16 us
    all_gather x4 -> x2, waiting for transfers between devices: 294 us -> 67.9 us  [the longest x1 48.7 us: shards(): gram_sum = lax.all_gather(sum_grams(grams, place, chunk), SHARD, axis=0)]
    all_to_all x4 -> x0, blocking collectives: 69.6 us -> none  [the longest x3 37.1 us: copy_for_each(): return lax.all_to_all(copies, axis, split_axis=0, concat_axis=0, tiled=True)]
    all_to_all x0 -> x3, waiting for transfers between devices: none -> 47.6 us  [exchange(): return lax.all_to_all(parts, axis, split_axis=0, concat_axis=0, tiled=True)]
    dot_general x4 -> x0, matrix products: 33.4 us -> none  [the longest x3 22.9 us: apply_gram(): jnp.dot(gram_sum, lax.all_gather(direction, 'shard', axis=0, tiled=True),...]
    ppermute x0 -> x23, waiting for transfers between devices: none -> 31.1 us  [the longest x21 17.5 us: turn(): lax.ppermute(block, axis, [(i, (i + step) % size) for i in range(size)])]
    dot_general x1 -> x0, local copies, waits for them, and re-layouts: 23.2 us -> none  [shards(): jnp.einsum('mrn,mno->ro', gram_low, lax.all_gather(member_weights, 'shard...]
    pallas_call x0 -> x4, Pallas kernels: none -> 22.2 us  [the longest x3 12.7 us: apply_gram(): pl.pallas_call(product_kernel, in_specs=[pl.BlockSpec(memory_space=pltpu....]
    ppermute x0 -> x23, starting transfers between devices: none -> 21.4 us  [the longest x21 14.3 us: turn(): lax.ppermute(block, axis, [(i, (i + step) % size) for i in range(size)])]
  transfers between devices with their start and end apart: 5 -> 28, of which waited for: 4 -> 14; matrix products, arithmetic and copies ran while one was open for 9% -> 12% of each run, Pallas kernels for 0% -> 4%
where the time goes in v1:
time: 267 us; the launch traced here: 266 us
  waiting for transfers between devices  147 us (55%)
  starting transfers between devices  38.8 us (15%)
  other arithmetic  27.1 us (10%)
  Pallas kernels  22.2 us (8%)
  local copies, waits for them, and re-layouts  16 us (6%)
  between operations  14 us (5%)
    all_gather x1, waiting for transfers between devices, shards(): gram_sum = lax.all_gather(sum_grams(grams, place, chunk), SHARD, axis=0)  48.7 us
    all_to_all x3, waiting for transfers between devices, exchange(): return lax.all_to_all(parts, axis, split_axis=0, concat_axis=0, tiled=True)  47.6 us
    all_gather x1, waiting for transfers between devices, shards(): weights = lax.all_gather(member_weights[0].T, MEMBER, axis=0)  19.2 us
    ppermute x21, waiting for transfers between devices, turn(): lax.ppermute(block, axis, [(i, (i + step) % size) for i in range(size)])  17.5 us
    all_to_all x3, starting transfers between devices, exchange(): return lax.all_to_all(parts, axis, split_axis=0, concat_axis=0, tiled=True)  17.3 us
    ppermute x21, starting transfers between devices, turn(): lax.ppermute(block, axis, [(i, (i + step) % size) for i in range(size)])  14.3 us
    reduce_sum x11, other arithmetic, column_sums(): return jnp.sum(a * b, axis=1, keepdims=True)  13.8 us
    ppermute x2, waiting for transfers between devices, to_output(): came.append(lax.ppermute(sent, ALL, pairs))  13.7 us
  transfers between devices with their start and end apart: 28, of which 14 were waited for; matrix products, arithmetic and copies ran while one was open for 12% of the time, Pallas kernels for 4%

profile of v1, /device:TPU:24, one launch (start us, length us, event | category | flops | bytes accessed | tf_op | source)
XLA Modules:
  0.0 265.5 jit_solution(3294324693403866635)
XLA Ops:
  7.3 3.3 %fusion.1 = (bf16[256,4096]{1,0:T(8,128)(2,1)S(1)}, bf16[4096]{0:T(1024)(128)(2,1)S(1)}) fusion(f32[1,256,4096]{2,1,0:T(8,128)} %param.2, s32[256]{0:T(256)S(1)} %iota_add_fusion.1), kind=kLoop, calls=%fused_computation.7 | loop fusion | flops 8384512 | bytes 6300672 | tf_op jit(solution)/shard_map/convert_element_type | solution.py:40
  10.9 1.5 copy.17
  12.4 4.7 %all-to-all-start = ((bf16[8,264,512]{2,1,0:T(8,128)(2,1)}), bf16[8,264,512]{2,1,0:T(8,128)(2,1)S(1)}, u32[]{:S(2)}, u32[]{:S(2)}) async-start(bf16[8,264,512]{2,1,0:T(8,128)(2,1)} %bitcast.51), calls=%async_computation | async-start | bytes 4325376 | tf_op jit(solution)/shard_map/all_to_all | solution.py:23
  17.1 44.3 %all-to-all-done.g_ref = bf16[8,264,512]{2,1,0:T(8,128)(2,1)S(1)} async-done(((bf16[8,264,512]{2,1,0:T(8,128)(2,1)}), bf16[8,264,512]{2,1,0:T(8,128)(2,1)S(1)}, u32[]{:S(2)}, u32[]{:S(2)}) %all-to-all-start) | async-done | bytes 2162720 | tf_op jit(solution)/shard_map/all_to_all | solution.py:23
  62.8 19.2 %all-gather.5.cloned.1.call-done = bf16[18432,256]{0,1:T(8,128)(2,1)} async-done(((bf16[2304,256]{0,1:T(8,128)(2,1)}), bf16[18432,256]{0,1:T(8,128)(2,1)}) %all-gather.5.cloned.1.call-update) | async-done | bytes 9437200 | tf_op jit(solution)/shard_map/all_gather | solution.py:139
  82.0 12.7 %copy.9 = bf16[18432,256]{1,0:T(8,128)(2,1)} copy(bf16[18432,256]{0,1:T(8,128)(2,1)} %all-gather.5.cloned.1.call-done) | data formatting | bytes 18874368 | tf_op jit(solution)/shard_map/all_gather | solution.py:139
  94.7 9.5 %right_side.1 = bf16[16,144,512]{2,1,0:T(8,128)(2,1)} custom-call(bf16[8,2304,256]{2,1,0:T(8,128)(2,1)} %bitcast.50, bf16[8,264,512]{2,1,0:T(8,128)(2,1)} %copy-done), custom_call_target="tpu_custom_call" | custom-call | tf_op jit(solution)/shard_map/right_side/pallas_call | solution.py:68
  104.2 7.9 %all-to-all-start.1 = ((bf16[16,144,512]{2,1,0:T(8,128)(2,1)}), bf16[16,144,512]{2,1,0:T(8,128)(2,1)S(1)}, u32[]{:S(2)}, u32[]{:S(2)}) async-start(bf16[16,144,512]{2,1,0:T(8,128)(2,1)} %right_side.1), calls=%async_computation.1 | async-start | bytes 4718592 | tf_op jit(solution)/shard_map/all_to_all | solution.py:23
  112.7 48.7 %all-gather.7.cloned.1.call-done = bf16[4224,512]{1,0:T(8,128)(2,1)} async-done(((bf16[264,512]{1,0:T(8,128)(2,1)}), bf16[4224,512]{1,0:T(8,128)(2,1)}) %all-gather.7.cloned.1.call-update) | async-done | bytes 4325392 | tf_op jit(solution)/shard_map/all_gather | solution.py:141
  161.4 2.2 dynamic-slice_convert_fusion
  164.9 2.9 %collective-permute-start.1 = (bf16[144,512]{1,0:T(8,128)(2,1)S(1)}, bf16[144,512]{1,0:T(8,128)(2,1)S(1)}, u32[]{:S(2)}, u32[]{:S(2)}) collective-permute-start(bf16[144,512]{1,0:T(8,128)(2,1)S(1)} %convert_element_type.113.refs_0_), channel_id=1, source_target_pairs={{0,64},{32,96},{64,0},{96,32},{1,65},{33,97},{65,1},{97,33},{2,66}... | collective-permute-start | bytes 442376 | tf_op jit(solution)/shard_map/ppermute | solution.py:28
  171.4 3.0 %collective-permute-done.1.refs_2_ = bf16[144,512]{1,0:T(8,128)(2,1)S(1)} collective-permute-done((bf16[144,512]{1,0:T(8,128)(2,1)S(1)}, bf16[144,512]{1,0:T(8,128)(2,1)S(1)}, u32[]{:S(2)}, u32[]{:S(2)}) %collective-permute-start.1) | collective-permute-done | bytes 147488 | tf_op jit(solution)/shard_map/ppermute | solution.py:28
  177.1 4.2 %apply_gram.3.own_ref = f32[144,512]{1,0:T(8,128)} custom-call(s32[2]{0:T(128)} %pad_add_fusion.pos_ref, bf16[16,264,512]{2,1,0:T(8,128)(2,1)} %bitcast.47, f32[8,512]{1,0:T(8,128)} %select_maximum_fusion.diag_ref, f32[144,512]{1,0:T(8,128)} %copy-done.1, bf16[144,512]{1,0:T(8,128)(2,1)} %copy-done.34, bf16[144,512]{1,0:T(8,128)(2,1)} %copy-done.11, ...), custom_call_target="tpu_custom_call" | custom-call | tf_op jit(solution)/shard_map/apply_gram/pallas_call | solution.py:94
  181.3 1.2 fusion.5
  183.3 2.8 %collective-permute-start.8 = (bf16[144,512]{1,0:T(8,128)(2,1)S(1)}, bf16[144,512]{1,0:T(8,128)(2,1)S(1)}, u32[]{:S(2)}, u32[]{:S(2)}) collective-permute-start(bf16[144,512]{1,0:T(8,128)(2,1)S(1)} %get-tuple-element.65.refs_0_), channel_id=1, source_target_pairs={{0,64},{32,96},{64,0},{96,32},{1,65},{33,97},{65,1},{97,33},{2,66}... | collective-permute-start | bytes 442376 | tf_op jit(solution)/shard_map/ppermute | solution.py:28
  186.5 3.2 %collective-permute-done.9.refs_3_ = bf16[144,512]{1,0:T(8,128)(2,1)S(1)} collective-permute-done((bf16[144,512]{1,0:T(8,128)(2,1)S(1)}, bf16[144,512]{1,0:T(8,128)(2,1)S(1)}, u32[]{:S(2)}, u32[]{:S(2)}) %collective-permute-start.9) | collective-permute-done | bytes 147488 | tf_op jit(solution)/shard_map/ppermute | solution.py:28
  190.9 2.6 collective-permute-done.8.refs_2_
  194.7 1.1 fusion.7
  199.9 1.2 fusion.15
  201.2 4.2 %apply_gram.4 = f32[144,512]{1,0:T(8,128)} custom-call(s32[2]{0:T(128)} %pad_add_fusion.pos_ref, bf16[16,264,512]{2,1,0:T(8,128)(2,1)} %bitcast.48, f32[8,512]{1,0:T(8,128)} %select_maximum_fusion.diag_ref, f32[144,512]{1,0:T(8,128)} %apply_gram.3.own_ref, bf16[144,512]{1,0:T(8,128)(2,1)} %copy-done.22, bf16[144,512]{1,0:T(8,128)(2,1)} %copy-done.20, ...), custom_call_target="tpu_custom_call" | custom-call | tf_op jit(solution)/shard_map/apply_gram/pallas_call | solution.py:94
  205.4 1.8 fusion.28
  207.2 2.5 collective-permute-start.15
  210.6 6.8 %collective-permute-done.16.refs_3_ = bf16[144,512]{1,0:T(8,128)(2,1)S(1)} collective-permute-done((bf16[144,512]{1,0:T(8,128)(2,1)S(1)}, bf16[144,512]{1,0:T(8,128)(2,1)S(1)}, u32[]{:S(2)}, u32[]{:S(2)}) %collective-permute-start.16) | collective-permute-done | bytes 147488 | tf_op jit(solution)/shard_map/ppermute | solution.py:28
  219.0 1.4 multiply_reduce_fusion.3
  220.5 2.1 multiply_reduce_fusion.8
  222.7 4.2 %apply_gram.5 = f32[144,512]{1,0:T(8,128)} custom-call(s32[2]{0:T(128)} %pad_add_fusion.pos_ref, bf16[16,264,512]{2,1,0:T(8,128)(2,1)} %bitcast.49, f32[8,512]{1,0:T(8,128)} %select_maximum_fusion.diag_ref, f32[144,512]{1,0:T(8,128)} %get-tuple-element.61.own_ref, bf16[144,512]{1,0:T(8,128)(2,1)} %copy-done.6, bf16[144,512]{1,0:T(8,128)(2,1)} %copy-done.31, ...), custom_call_target="tpu_custom_call" | custom-call | tf_op jit(solution)/shard_map/apply_gram/pallas_call | solution.py:94
  227.0 1.3 multiply_reduce_fusion.1
  228.9 4.8 %all-to-all-start.2 = ((f32[8,1,2,144]{3,2,1,0:T(2,128)}), f32[8,1,2,144]{3,2,1,0:T(2,128)S(1)}, u32[]{:S(2)}, u32[]{:S(2)}) async-start(f32[8,1,2,144]{3,2,1,0:T(2,128)} %broadcast_in_dim.31), calls=%async_computation.2 | async-start | bytes 32768 | tf_op jit(solution)/shard_map/all_to_all | solution.py:23
  233.6 3.3 %all-to-all-done.2 = f32[8,1,2,144]{3,2,1,0:T(2,128)S(1)} async-done(((f32[8,1,2,144]{3,2,1,0:T(2,128)}), f32[8,1,2,144]{3,2,1,0:T(2,128)S(1)}, u32[]{:S(2)}, u32[]{:S(2)}) %all-to-all-start.2) | async-done | bytes 9248 | tf_op jit(solution)/shard_map/all_to_all | solution.py:23
  237.2 4.5 %collective-permute-start.21 = (f32[144,256]{1,0:T(8,128)S(1)}, f32[144,256]{1,0:T(8,128)S(1)}, u32[]{:S(2)}, u32[]{:S(2)}) collective-permute-start(f32[144,256]{1,0:T(8,128)S(1)} %get-tuple-element.72), channel_id=1, source_target_pairs={{0,0},{1,1},{2,16},{3,17},{4,32},{5,33},{6,48},{7,49},{8,64},{9,65... | collective-permute-start | bytes 442376 | tf_op jit(solution)/shard_map/ppermute | solution.py:119
  241.7 2.6 collective-permute-start.22
  244.3 13.7 %collective-permute-done.21 = f32[144,256]{1,0:T(8,128)S(1)} collective-permute-done((f32[144,256]{1,0:T(8,128)S(1)}, f32[144,256]{1,0:T(8,128)S(1)}, u32[]{:S(2)}, u32[]{:S(2)}) %collective-permute-start.21) | collective-permute-done | bytes 147488 | tf_op jit(solution)/shard_map/ppermute | solution.py:119
  (146 shorter events, 22.3 us)
Async XLA Ops:
  6.5 75.5 %all-gather.5.cloned.1.call-start = ((), (), s32[]{:S(2)}) async-start(), calls=%async_computation.3 | async-start | bytes 10616832 | tf_op jit(solution)/shard_map/all_gather | solution.py:139
  12.4 49.0 %all-to-all-start = ((bf16[8,264,512]{2,1,0:T(8,128)(2,1)}), bf16[8,264,512]{2,1,0:T(8,128)(2,1)S(1)}, u32[]{:S(2)}, u32[]{:S(2)}) async-start(bf16[8,264,512]{2,1,0:T(8,128)(2,1)} %bitcast.51), calls=%async_computation | async-start | bytes 4325376 | tf_op jit(solution)/shard_map/all_to_all | solution.py:23
  17.0 144.3 %all-gather.7.cloned.1.call-start = ((), (), s32[]{:S(2)}) async-start(), calls=%async_computation.4 | async-start | bytes 4595712 | tf_op jit(solution)/shard_map/all_gather | solution.py:141
  61.4 33.3 %copy-start = (bf16[8,264,512]{2,1,0:T(8,128)(2,1)}, bf16[8,264,512]{2,1,0:T(8,128)(2,1)S(1)}, u32[]{:S(2)}) copy-start(bf16[8,264,512]{2,1,0:T(8,128)(2,1)S(1)} %all-to-all-done.g_ref) | copy-start | bytes 6488068
  104.2 59.3 %all-to-all-start.1 = ((bf16[16,144,512]{2,1,0:T(8,128)(2,1)}), bf16[16,144,512]{2,1,0:T(8,128)(2,1)S(1)}, u32[]{:S(2)}, u32[]{:S(2)}) async-start(bf16[16,144,512]{2,1,0:T(8,128)(2,1)} %right_side.1), calls=%async_computation.1 | async-start | bytes 4718592 | tf_op jit(solution)/shard_map/all_to_all | solution.py:23
  163.9 7.4 %collective-permute-start.2 = (bf16[144,512]{1,0:T(8,128)(2,1)S(1)}, bf16[144,512]{1,0:T(8,128)(2,1)S(1)}, u32[]{:S(2)}, u32[]{:S(2)}) collective-permute-start(bf16[144,512]{1,0:T(8,128)(2,1)S(1)} %convert_element_type.113.refs_0_), channel_id=1, source_target_pairs={{0,96},{32,0},{64,32},{96,64},{1,97},{33,1},{65,33},{97,65},{2,98}... | collective-permute-start | bytes 442376 | tf_op jit(solution)/shard_map/ppermute | solution.py:28
  164.9 9.4 %collective-permute-start.1 = (bf16[144,512]{1,0:T(8,128)(2,1)S(1)}, bf16[144,512]{1,0:T(8,128)(2,1)S(1)}, u32[]{:S(2)}, u32[]{:S(2)}) collective-permute-start(bf16[144,512]{1,0:T(8,128)(2,1)S(1)} %convert_element_type.113.refs_0_), channel_id=1, source_target_pairs={{0,64},{32,96},{64,0},{96,32},{1,65},{33,97},{65,1},{97,33},{2,66}... | collective-permute-start | bytes 442376 | tf_op jit(solution)/shard_map/ppermute | solution.py:28
  167.9 6.5 %collective-permute-start = (bf16[144,512]{1,0:T(8,128)(2,1)S(1)}, bf16[144,512]{1,0:T(8,128)(2,1)S(1)}, u32[]{:S(2)}, u32[]{:S(2)}) collective-permute-start(bf16[144,512]{1,0:T(8,128)(2,1)S(1)} %convert_element_type.113.refs_0_), channel_id=1, source_target_pairs={{0,32},{32,64},{64,96},{96,0},{1,33},{33,65},{65,97},{97,1},{2,34}... | collective-permute-start | bytes 442376 | tf_op jit(solution)/shard_map/ppermute | solution.py:28
  170.4 5.1 %collective-permute-start.3 = (bf16[144,512]{1,0:T(8,128)(2,1)S(1)}, bf16[144,512]{1,0:T(8,128)(2,1)S(1)}, u32[]{:S(2)}, u32[]{:S(2)}) collective-permute-start(bf16[144,512]{1,0:T(8,128)(2,1)S(1)} %convert_element_type.113.refs_0_), channel_id=1, source_target_pairs={{0,16},{16,0},{1,17},{17,1},{2,18},{18,2},{3,19},{19,3},{4,20},{20... | collective-permute-start | bytes 442376 | tf_op jit(solution)/shard_map/ppermute | solution.py:28
  171.4 4.1 %collective-permute-start.6 = (bf16[144,512]{1,0:T(8,128)(2,1)S(1)}, bf16[144,512]{1,0:T(8,128)(2,1)S(1)}, u32[]{:S(2)}, u32[]{:S(2)}) collective-permute-start(bf16[144,512]{1,0:T(8,128)(2,1)S(1)} %collective-permute-done.2.refs_3_), channel_id=1, source_target_pairs={{0,16},{16,0},{1,17},{17,1},{2,18},{18,2},{3,19},{19,3},{4,20},{20... | collective-permute-start | bytes 442376 | tf_op jit(solution)/shard_map/ppermute | solution.py:28
  174.4 1.4 collective-permute-start.5
  174.4 1.6 collective-permute-start.4
  182.5 22.9 %copy-start.3 = (f32[144,512]{1,0:T(8,128)S(1)}, f32[144,512]{1,0:T(8,128)}, u32[]{:S(2)}) copy-start(f32[144,512]{1,0:T(8,128)} %apply_gram.3.own_ref) | copy-start | bytes 884740
  182.5 7.2 %collective-permute-start.9 = (bf16[144,512]{1,0:T(8,128)(2,1)S(1)}, bf16[144,512]{1,0:T(8,128)(2,1)S(1)}, u32[]{:S(2)}, u32[]{:S(2)}) collective-permute-start(bf16[144,512]{1,0:T(8,128)(2,1)S(1)} %get-tuple-element.65.refs_0_), channel_id=1, source_target_pairs={{0,96},{32,0},{64,32},{96,64},{1,97},{33,1},{65,33},{97,65},{2,98}... | collective-permute-start | bytes 442376 | tf_op jit(solution)/shard_map/ppermute | solution.py:28
  183.3 10.2 %collective-permute-start.8 = (bf16[144,512]{1,0:T(8,128)(2,1)S(1)}, bf16[144,512]{1,0:T(8,128)(2,1)S(1)}, u32[]{:S(2)}, u32[]{:S(2)}) collective-permute-start(bf16[144,512]{1,0:T(8,128)(2,1)S(1)} %get-tuple-element.65.refs_0_), channel_id=1, source_target_pairs={{0,64},{32,96},{64,0},{96,32},{1,65},{33,97},{65,1},{97,33},{2,66}... | collective-permute-start | bytes 442376 | tf_op jit(solution)/shard_map/ppermute | solution.py:28
  186.1 10.3 %collective-permute-start.10 = (bf16[144,512]{1,0:T(8,128)(2,1)S(1)}, bf16[144,512]{1,0:T(8,128)(2,1)S(1)}, u32[]{:S(2)}, u32[]{:S(2)}) collective-permute-start(bf16[144,512]{1,0:T(8,128)(2,1)S(1)} %get-tuple-element.65.refs_0_), channel_id=1, source_target_pairs={{0,16},{16,0},{1,17},{17,1},{2,18},{18,2},{3,19},{19,3},{4,20},{20... | collective-permute-start | bytes 442376 | tf_op jit(solution)/shard_map/ppermute | solution.py:28
  186.1 8.6 %collective-permute-start.7 = (bf16[144,512]{1,0:T(8,128)(2,1)S(1)}, bf16[144,512]{1,0:T(8,128)(2,1)S(1)}, u32[]{:S(2)}, u32[]{:S(2)}) collective-permute-start(bf16[144,512]{1,0:T(8,128)(2,1)S(1)} %get-tuple-element.65.refs_0_), channel_id=1, source_target_pairs={{0,32},{32,64},{64,96},{96,0},{1,33},{33,65},{65,97},{97,1},{2,34}... | collective-permute-start | bytes 442376 | tf_op jit(solution)/shard_map/ppermute | solution.py:28
  190.8 6.7 %collective-permute-start.13 = (bf16[144,512]{1,0:T(8,128)(2,1)S(1)}, bf16[144,512]{1,0:T(8,128)(2,1)S(1)}, u32[]{:S(2)}, u32[]{:S(2)}) collective-permute-start(bf16[144,512]{1,0:T(8,128)(2,1)S(1)} %collective-permute-done.9.refs_3_), channel_id=1, source_target_pairs={{0,16},{16,0},{1,17},{17,1},{2,18},{18,2},{3,19},{19,3},{4,20},{20... | collective-permute-start | bytes 442376 | tf_op jit(solution)/shard_map/ppermute | solution.py:28
  194.6 4.1 %collective-permute-start.12 = (bf16[144,512]{1,0:T(8,128)(2,1)S(1)}, bf16[144,512]{1,0:T(8,128)(2,1)S(1)}, u32[]{:S(2)}, u32[]{:S(2)}) collective-permute-start(bf16[144,512]{1,0:T(8,128)(2,1)S(1)} %collective-permute-done.8.refs_2_), channel_id=1, source_target_pairs={{0,16},{16,0},{1,17},{17,1},{2,18},{18,2},{3,19},{19,3},{4,20},{20... | collective-permute-start | bytes 442376 | tf_op jit(solution)/shard_map/ppermute | solution.py:28
  195.8 23.1 %copy-start.24 = (bf16[144,512]{1,0:T(8,128)(2,1)S(1)}, bf16[144,512]{1,0:T(8,128)(2,1)}, u32[]{:S(2)}) copy-start(bf16[144,512]{1,0:T(8,128)(2,1)} %copy-done.23) | copy-start | bytes 442372
  195.9 23.1 %copy-start.26 = (bf16[144,512]{1,0:T(8,128)(2,1)S(1)}, bf16[144,512]{1,0:T(8,128)(2,1)}, u32[]{:S(2)}) copy-start(bf16[144,512]{1,0:T(8,128)(2,1)} %copy-done.25) | copy-start | bytes 442372
  195.9 4.0 %collective-permute-start.11 = (bf16[144,512]{1,0:T(8,128)(2,1)S(1)}, bf16[144,512]{1,0:T(8,128)(2,1)S(1)}, u32[]{:S(2)}, u32[]{:S(2)}) collective-permute-start(bf16[144,512]{1,0:T(8,128)(2,1)S(1)} %collective-permute-done.7.refs_1_), channel_id=1, source_target_pairs={{0,16},{16,0},{1,17},{17,1},{2,18},{18,2},{3,19},{19,3},{4,20},{20... | collective-permute-start | bytes 442376 | tf_op jit(solution)/shard_map/ppermute | solution.py:28
  207.2 10.2 %collective-permute-start.16 = (bf16[144,512]{1,0:T(8,128)(2,1)S(1)}, bf16[144,512]{1,0:T(8,128)(2,1)S(1)}, u32[]{:S(2)}, u32[]{:S(2)}) collective-permute-start(bf16[144,512]{1,0:T(8,128)(2,1)S(1)} %get-tuple-element.60.refs_0_), channel_id=1, source_target_pairs={{0,96},{32,0},{64,32},{96,64},{1,97},{33,1},{65,33},{97,65},{2,98}... | collective-permute-start | bytes 442376 | tf_op jit(solution)/shard_map/ppermute | solution.py:28
  207.2 10.2 %collective-permute-start.15 = (bf16[144,512]{1,0:T(8,128)(2,1)S(1)}, bf16[144,512]{1,0:T(8,128)(2,1)S(1)}, u32[]{:S(2)}, u32[]{:S(2)}) collective-permute-start(bf16[144,512]{1,0:T(8,128)(2,1)S(1)} %get-tuple-element.60.refs_0_), channel_id=1, source_target_pairs={{0,64},{32,96},{64,0},{96,32},{1,65},{33,97},{65,1},{97,33},{2,66}... | collective-permute-start | bytes 442376 | tf_op jit(solution)/shard_map/ppermute | solution.py:28
  209.7 8.3 %collective-permute-start.14 = (bf16[144,512]{1,0:T(8,128)(2,1)S(1)}, bf16[144,512]{1,0:T(8,128)(2,1)S(1)}, u32[]{:S(2)}, u32[]{:S(2)}) collective-permute-start(bf16[144,512]{1,0:T(8,128)(2,1)S(1)} %get-tuple-element.60.refs_0_), channel_id=1, source_target_pairs={{0,32},{32,64},{64,96},{96,0},{1,33},{33,65},{65,97},{97,1},{2,34}... | collective-permute-start | bytes 442376 | tf_op jit(solution)/shard_map/ppermute | solution.py:28
  217.4 1.4 collective-permute-start.20
  217.4 1.6 collective-permute-start.19
  217.9 2.5 collective-permute-start.17
  218.0 2.4 collective-permute-start.18
  228.9 8.0 %all-to-all-start.2 = ((f32[8,1,2,144]{3,2,1,0:T(2,128)}), f32[8,1,2,144]{3,2,1,0:T(2,128)S(1)}, u32[]{:S(2)}, u32[]{:S(2)}) async-start(f32[8,1,2,144]{3,2,1,0:T(2,128)} %broadcast_in_dim.31), calls=%async_computation.2 | async-start | bytes 32768 | tf_op jit(solution)/shard_map/all_to_all | solution.py:23
  237.2 20.8 %collective-permute-start.21 = (f32[144,256]{1,0:T(8,128)S(1)}, f32[144,256]{1,0:T(8,128)S(1)}, u32[]{:S(2)}, u32[]{:S(2)}) collective-permute-start(f32[144,256]{1,0:T(8,128)S(1)} %get-tuple-element.72), channel_id=1, source_target_pairs={{0,0},{1,1},{2,16},{3,17},{4,32},{5,33},{6,48},{7,49},{8,64},{9,65... | collective-permute-start | bytes 442376 | tf_op jit(solution)/shard_map/ppermute | solution.py:119
  241.7 16.3 %collective-permute-start.22 = (f32[144,256]{1,0:T(8,128)S(1)}, f32[144,256]{1,0:T(8,128)S(1)}, u32[]{:S(2)}, u32[]{:S(2)}) collective-permute-start(f32[144,256]{1,0:T(8,128)S(1)} %get-tuple-element.73), channel_id=1, source_target_pairs={{0,1},{1,0},{2,17},{3,16},{4,33},{5,32},{6,49},{7,48},{8,65},{9,64... | collective-permute-start | bytes 442376 | tf_op jit(solution)/shard_map/ppermute | solution.py:119
  (33 other events, 270.1 us)
Sparse Core Ops, SparseCore 0:
  9.0 72.9 all-gather.4
  84.2 77.1 all-gather.6
